TPU v7x, 128 devices: a whole 4x4x4 slice. The times are simulated.
128 devices in a mesh: front: 4 (over y), row: 4 (over z_lo, core), col: 8 (over x, z_hi).
Axes of the slice: x: 4, y: 4, z: 4 (z_hi: 2, z_lo: 2; z = z_hi * 2 + z_lo), core: 2. Of those that a mesh axis runs over, the one named last changes fastest.
Arguments:
- pivot_block: bfloat16 [4, 1024, 1024], P('front'), may hold values from -6 to 6
- border: bfloat16 [4, 8192, 1024], P('front', 'row'), may hold values from -6 to 6
- contrib: bfloat16 [4, 8192, 8192], P('front', 'row', 'col'), may hold values from -6 to 6
- inverses: bfloat16 [4, 4, 256, 256], P('front'), may hold values from -0.0625 to 0.0625
- row_tiles: int32 [4, 64], replicated, may hold values from 0 to 79, as said below
- col_tiles: int32 [4, 64], replicated, may hold values from 0 to 79, as said below
- owner: int32 [80], replicated, may hold values from 0 to 79, as said below
- schur_init: bfloat16 [10240, 10240], P(('front', 'row'), 'col'), may hold values from -6 to 6
- block: bfloat16 [10240, 512], P('col'), may hold values from -0.0625 to 0.0625
Outputs:
- schur: float32 [10240, 10240], P(('front', 'row'), 'col')
- product: float32 [10240, 512], P(('front', 'row', 'col'))
Inputs may be any that keep to these rules, and one draw needn't show every extreme that they name: owner is a permutation of 0 .. 79. For each front the 64 entries are distinct. With s = owner[row_tiles[f, i]], each front has exactly 4 entries in each group s // 5; among the 16 entries of one aligned block of a front at most 2 fall in one group, and that many in some block of every draw. For each front the 64 entries are distinct. With s = owner[col_tiles[f, j]], each front has exactly 8 entries in each group s // 10; among the 8 entries of one aligned block of a front at most 2 fall in one group, and that many in some block of every draw.
All inputs are finite; a program needn't handle non-finite values.
Results may differ from a plain program's by a relative error of at most 0.008.
Values may be sent and summed in bfloat16 or wider, within the bound.
A program may use at most 128 MiB of HBM per device.

v0:
```python
import jax
import jax.numpy as jnp
from jax import lax
from jax.sharding import PartitionSpec as P

TILE = 128


def in_blocks(x, dim, length):
    before, after = (x.shape[:dim], x.shape[dim + 1 :])
    return jnp.moveaxis(x.reshape(*before, length, -1, *after), dim, 0)


def sent_and_summed(x, axis, dim):
    tiles = in_blocks(x, dim, lax.axis_size(axis))
    arrived = lax.all_to_all(tiles, axis, split_axis=0, concat_axis=0, tiled=True)
    return arrived.sum(axis=0)


def eliminate(pivot, rows, inverse_set):
    panels = inverse_set.shape[0]
    width = inverse_set.shape[1]
    pivot_now = pivot.astype(jnp.float32)
    rows_now = rows.astype(jnp.float32)
    leaves = []
    for panel_index in range(panels):
        start = panel_index * width
        left = pivot_now[:, start : start + width].astype(jnp.bfloat16)
        below = jnp.arange(pivot.shape[0])[:, None] >= start + width
        lower = jnp.where(
            below, jnp.dot(left, inverse_set[panel_index], preferred_element_type=jnp.float32), 0.0
        ).astype(jnp.bfloat16)
        side = jnp.dot(
            rows_now[:, start : start + width].astype(jnp.bfloat16),
            inverse_set[panel_index],
            preferred_element_type=jnp.float32,
        ).astype(jnp.bfloat16)
        pivot_now = pivot_now - lax.dot_general(
            lower, lower, (((1,), (1,)), ((), ())), preferred_element_type=jnp.float32
        )
        rows_now = rows_now - lax.dot_general(
            side, lower, (((1,), (1,)), ((), ())), preferred_element_type=jnp.float32
        )
        leaves.append(side)
    return jnp.concatenate(leaves, axis=1)


def route_tables(slots, per_group):
    group = slots // per_group
    within = slots % per_group
    count = slots.shape[-1]
    same = group[..., :, None] == group[..., None, :]
    earlier = jnp.arange(count)[None, :] < jnp.arange(count)[:, None]
    rank = jnp.sum((same & earlier).astype(jnp.int32), axis=-1)
    return (group, rank, within)


def pick_sources(group, rank, n_groups, capacity):
    count = group.shape[-1]
    match = (group[None, None, :] == jnp.arange(n_groups)[:, None, None]) & (
        rank[None, None, :] == jnp.arange(capacity)[None, :, None]
    )
    return jnp.sum(match.astype(jnp.int32) * jnp.arange(count)[None, None, :], axis=-1)


def shards(pivot_block, border, contrib, inverses, row_tiles, col_tiles, owner, schur_init, block):
    n_front = lax.axis_size("front")
    n_row = lax.axis_size("row")
    n_col = lax.axis_size("col")
    front_index = lax.axis_index("front")
    row_index = lax.axis_index("row")
    col_index = lax.axis_index("col")
    groups = n_front * n_row
    tiles_all = row_tiles.shape[1]
    slots_all = owner.shape[0]
    row_span = border.shape[1]
    col_span = contrib.shape[2]
    tile_rows = row_span // TILE
    tile_cols = col_span // TILE
    rows_per_group = slots_all // groups
    cols_per_group = slots_all // n_col
    cap_rows = 2 * tiles_all // (n_row * groups)
    cap_cols = 2 * tiles_all // (n_col * n_col)
    share = row_span // n_col
    own_rows = lax.dynamic_slice_in_dim(border[0], col_index * share, share, 0)
    leaves = eliminate(pivot_block[0], own_rows, inverses[0])
    factor = lax.all_gather(leaves, ("row", "col"), axis=0, tiled=True)
    mine = lax.dynamic_slice_in_dim(factor, row_index * row_span, row_span, 0)
    theirs = lax.dynamic_slice_in_dim(factor, col_index * col_span, col_span, 0)
    update = (
        contrib[0].astype(jnp.float32)
        - lax.dot_general(
            mine, theirs, (((1,), (1,)), ((), ())), preferred_element_type=jnp.float32
        )
    ).astype(jnp.bfloat16)
    tiles = update.reshape(tile_rows, TILE, tile_cols, TILE)
    slot_rows = owner[row_tiles].reshape(n_front, n_row, tile_rows)
    slot_cols = owner[col_tiles].reshape(n_front, n_col, tile_cols)
    group_rows, rank_rows, within_rows = route_tables(slot_rows, rows_per_group)
    group_cols, rank_cols, within_cols = route_tables(slot_cols, cols_per_group)
    send_rows = pick_sources(
        group_rows[front_index, row_index], rank_rows[front_index, row_index], groups, cap_rows
    )
    my_group = front_index * n_row + row_index
    flat_group = group_rows.reshape(groups, tile_rows)
    flat_rank = rank_rows.reshape(groups, tile_rows)
    flat_within = within_rows.reshape(groups, tile_rows)
    hit_rows = (flat_group == my_group)[:, None, :] & (
        flat_rank[:, None, :] == jnp.arange(cap_rows)[None, :, None]
    )
    place_rows = jnp.sum(
        (
            hit_rows[None]
            & (flat_within[None, :, None, :] == jnp.arange(rows_per_group)[:, None, None, None])
        ).astype(jnp.int32),
        axis=-1,
    ).astype(jnp.bfloat16)
    hit_cols = (group_cols == col_index)[:, :, None, :] & (
        rank_cols[:, :, None, :] == jnp.arange(cap_cols)[None, None, :, None]
    )
    place_cols = jnp.sum(
        (
            hit_cols[None]
            & (
                within_cols[None, :, :, None, :]
                == jnp.arange(cols_per_group)[:, None, None, None, None]
            )
        ).astype(jnp.int32),
        axis=-1,
    ).astype(jnp.bfloat16)
    place_cols = jnp.repeat(place_cols, n_row, axis=1)
    send_cols = pick_sources(
        group_cols[front_index, col_index], rank_cols[front_index, col_index], n_col, cap_cols
    )
    by_rows = jnp.take(tiles, send_rows.reshape(-1), axis=0)
    by_both = jnp.take(by_rows, send_cols.reshape(-1), axis=2)
    outgoing = by_both.reshape(groups, cap_rows, TILE, n_col, cap_cols, TILE).transpose(
        0, 3, 1, 4, 2, 5
    )
    outgoing = outgoing.reshape(groups * n_col, cap_rows, cap_cols, TILE, TILE)
    received = lax.all_to_all(
        outgoing, ("front", "row", "col"), split_axis=0, concat_axis=0, tiled=True
    )
    received = received.reshape(groups, n_col, cap_rows, cap_cols, TILE, TILE)
    gathered = jnp.einsum(
        "bgcm,gckmxy->bgkxy", place_cols, received, preferred_element_type=jnp.float32
    ).astype(jnp.bfloat16)
    summed = jnp.einsum("agk,bgkxy->abxy", place_rows, gathered, preferred_element_type=jnp.float32)
    schur = schur_init.astype(jnp.float32) + summed.transpose(0, 2, 1, 3).reshape(
        rows_per_group * TILE, cols_per_group * TILE
    )
    rounded = schur.astype(jnp.bfloat16)
    product = sent_and_summed(jnp.dot(rounded, block, preferred_element_type=jnp.float32), "col", 0)
    return (schur, product)


def solution(mesh):
    in_specs = (
        P("front", None, None),
        P("front", "row", None),
        P("front", "row", "col"),
        P("front", None, None, None),
        P(),
        P(),
        P(),
        P(("front", "row"), "col"),
        P("col", None),
    )
    out_specs = (P(("front", "row"), "col"), P(("front", "row", "col"), None))
    return jax.shard_map(shards, mesh=mesh, in_specs=in_specs, out_specs=out_specs, check_vma=False)
```

profile of v0, /device:TPU:0, one launch (start us, length us, event | category | flops | bytes accessed | tf_op | source)
XLA Modules:
  0.0 539.3 jit_solution(2947707500783428051)
XLA Ops:
  7.3 1.2 dynamic-slice_bitcast_fusion
  8.5 1.1 convolution_convert_fusion.3
  9.7 1.4 fusion.19
  12.8 2.7 fusion.59
  16.7 2.2 fusion.22
  18.9 1.1 convolution_convert_fusion
  20.1 1.8 pad_maximum_fusion
  22.0 2.0 gather_fusion
  25.3 1.9 gather_fusion.1
  28.7 117.7 %all-gather.2.cloned.1.call-done = bf16[8192,1024]{0,1:T(8,128)(2,1)} async-done(((bf16[256,1024]{0,1:T(8,128)(2,1)}), bf16[8192,1024]{0,1:T(8,128)(2,1)}) %all-gather.2.cloned.1.call-update) | async-done | bytes 16777232 | tf_op jit(solution)/shard_map/all_gather | solution.py:87
  146.4 8.7 %fusion.8 = bf16[256,8,8,128]{3,1,2,0:T(8,128)(2,1)S(1)} fusion(bf16[1,2048,1024]{2,1,0:T(8,128)(2,1)} %param.11, bf16[8192,1024]{0,1:T(8,128)(2,1)} %all-gather.2.cloned.1.call-done, s32[]{:T(128)S(6)} %select_n.153, s32[]{:T(128)S(6)} %select_n.154), kind=kOutput, calls=%fused_computation.14 | convolution fusion | flops 4301258752 | bytes 14680072 | tf_op jit(solution)/shard_map/dot_general | solution.py:92
  155.1 3.1 copy.39
  158.2 7.2 %gather_fusion.2 = bf16[32,128,8,128]{3,2,1,0:T(8,128)(2,1)} fusion(bf16[16,128,8,128]{3,2,1,0:T(8,128)(2,1)} %bitcast.87, s32[1024]{0:T(1024)S(1)} %pad_clamp_fusion.1), kind=kCustom, calls=%fused_computation.2 | custom fusion | bytes 16777344 | tf_op jit(solution)/shard_map/jit(_take)/gather | solution.py:135
  165.4 7.5 %broadcast_select_fusion = bf16[32,128,8,128]{3,2,1,0:T(8,128)(2,1)} fusion(bf16[32,128,8,128]{3,2,1,0:T(8,128)(2,1)} %gather_fusion.2, pred[32]{0:T(512)(128)(4,1)S(1)} %compare_and_fusion.2), kind=kLoop, calls=%fused_computation.13 | loop fusion | flops 4194304 | bytes 16777248 | tf_op jit(solution)/shard_map/jit(_take)/select_n | solution.py:135
  172.8 8.8 %copy.26 = bf16[32,128,8,128]{3,1,0,2:T(8,128)(2,1)} copy(bf16[32,128,8,128]{3,2,1,0:T(8,128)(2,1)} %broadcast_select_fusion) | data formatting | bytes 16777216 | tf_op jit(solution)/shard_map/jit(_take)/select_n | solution.py:135
  181.7 10.4 %gather_fusion.3 = bf16[16,32,128,128]{3,2,1,0:T(8,128)(2,1)} fusion(bf16[32,128,8,128]{3,1,0,2:T(8,128)(2,1)} %copy.26, s32[1024]{0:T(1024)S(1)} %pad_clamp_fusion), kind=kCustom, calls=%fused_computation.3 | custom fusion | bytes 33554496 | tf_op jit(solution)/shard_map/jit(_take)/gather | solution.py:136
  192.1 14.1 %copy_select_fusion = bf16[16,2,128,8,2,128]{5,2,4,1,3,0:T(8,128)(2,1)} fusion(bf16[16,2,128,8,2,128]{5,2,1,0,4,3:T(8,128)(2,1)} %bitcast.86, pred[8,2]{1,0:T(8,128)(4,1)S(1)} %copy.22), kind=kLoop, calls=%fused_computation.8 | loop fusion | flops 8388608 | bytes 33554448 | tf_op jit(solution)/shard_map/jit(_take)/select_n | solution.py:136
  206.2 11.1 %all-to-all-start = ((bf16[128,2,2,128,128]{4,3,2,1,0:T(8,128)(2,1)}), bf16[128,2,2,128,128]{4,3,2,1,0:T(8,128)(2,1)}, u32[]{:S(2)}, u32[]{:S(2)}) async-start(bf16[128,2,2,128,128]{4,3,2,1,0:T(8,128)(2,1)} %bitcast.85), calls=%async_computation | async-start | bytes 33554432 | tf_op jit(solution)/shard_map/all_to_all | solution.py:141
  218.2 235.2 %all-to-all-done = bf16[128,2,2,128,128]{4,3,2,1,0:T(8,128)(2,1)} async-done(((bf16[128,2,2,128,128]{4,3,2,1,0:T(8,128)(2,1)}), bf16[128,2,2,128,128]{4,3,2,1,0:T(8,128)(2,1)}, u32[]{:S(2)}, u32[]{:S(2)}) %all-to-all-start) | async-done | bytes 16777248 | tf_op jit(solution)/shard_map/all_to_all | solution.py:141
  453.4 25.6 %fusion = bf16[10,16,2,128,128]{4,0,3,2,1:T(8,128)(2,1)} fusion(bf16[10,16,8,2,1,1]{0,2,3,5,4,1:T(8,128)(2,1)S(1)} %bitcast.91, bf16[16,8,2,2,128,128]{5,4,3,2,1,0:T(8,128)(2,1)} %bitcast.19), kind=kOutput, calls=%fused_computation.5 | convolution fusion | flops 173015040 | bytes 27268096 | tf_op jit(solution)/shard_map/bgcm,gckmxy->bgkxy/dot_general | solution.py:145
  479.1 18.8 %fusion.11 = f32[5,128,10,128]{3,0,1,2:T(8,128)S(1)} fusion(bf16[10,16,2,128,128]{4,0,3,2,1:T(8,128)(2,1)} %fusion, bf16[5,16,2,1,1]{1,2,0,4,3:T(2,128)(2,1)S(1)} %convert_bitcast_fusion), kind=kOutput, calls=%fused_computation.19 | convolution fusion | flops 52428800 | bytes 13762880 | tf_op jit(solution)/shard_map/agk,bgkxy->abxy/dot_general | solution.py:148
  497.9 2.0 copy.32
  499.9 1.7 bitcast_add_fusion
  503.3 28.4 %all_to_all.10 = f32[8,80,512]{2,1,0:T(8,128)S(1)} all-to-all(f32[8,80,512]{2,1,0:T(8,128)S(1)} %bitcast.90), channel_id=1, replica_groups=mesh['front'=4,'row'=4,'col'=8] {'col'}, dimensions={0} | all-to-all | bytes 2621440 | tf_op jit(solution)/shard_map/all_to_all | solution.py:16
  (91 shorter events, 9.1 us)
Async XLA Ops:
  7.2 494.4 %copy-start = (bf16[1280,512]{1,0:T(8,128)(2,1)S(1)}, bf16[1280,512]{1,0:T(8,128)(2,1)}, u32[]{:S(2)}) copy-start(bf16[1280,512]{1,0:T(8,128)(2,1)} %param.17) | copy-start | bytes 3932164
  7.2 3.9 copy-start.4
  7.2 139.2 %all-gather.2.cloned.1.call-start = ((), (), s32[]{:S(2)}) async-start(), calls=%async_computation.2 | async-start | bytes 17301504 | tf_op jit(solution)/shard_map/all_gather | solution.py:87
  11.1 1.1 copy-start.6
  11.8 3.7 copy-start.2
  12.4 3.4 copy-start.7
  15.5 6.4 %copy-start.8 = (s32[4,64]{1,0:T(4,128)S(1)}, s32[4,64]{1,0:T(4,128)}, u32[]{:S(2)}) copy-start(s32[4,64]{1,0:T(4,128)} %param.14) | copy-start | bytes 3076
  15.5 6.4 %copy-start.9 = (s32[4,64]{1,0:T(4,128)S(1)}, s32[4,64]{1,0:T(4,128)}, u32[]{:S(2)}) copy-start(s32[4,64]{1,0:T(4,128)} %param.13) | copy-start | bytes 3076
  15.5 6.5 %copy-start.1 = (s32[80]{0:T(128)S(1)}, s32[80]{0:T(128)}, u32[]{:S(2)}) copy-start(s32[80]{0:T(128)} %param.15) | copy-start | bytes 964
  206.2 247.2 %all-to-all-start = ((bf16[128,2,2,128,128]{4,3,2,1,0:T(8,128)(2,1)}), bf16[128,2,2,128,128]{4,3,2,1,0:T(8,128)(2,1)}, u32[]{:S(2)}, u32[]{:S(2)}) async-start(bf16[128,2,2,128,128]{4,3,2,1,0:T(8,128)(2,1)} %bitcast.85), calls=%async_computation | async-start | bytes 33554432 | tf_op jit(solution)/shard_map/all_to_all | solution.py:141
  497.9 2.0 copy-start.5
  501.6 1.7 copy-start.3
Sparse Core Ops, SparseCore 0:
  22.0 124.3 all-gather.1
where the time goes:
time: 540 us; the launch traced here: 539 us
  waiting for transfers between devices  353 us (65%)
  matrix products  65.5 us (12%)
  local copies, waits for them, and re-layouts  38.8 us (7%)
  blocking collectives  28.4 us (5%)
  other arithmetic  28 us (5%)
  between operations  14.5 us (3%)
  starting transfers between devices  11.1 us (2%)
    all_to_all x1, waiting for transfers between devices, shards(): lax.all_to_all(outgoing, ('front', 'row', 'col'), split_axis=0, concat_ax...  235 us
    all_gather x1, waiting for transfers between devices, shards(): factor = lax.all_gather(leaves, ('row', 'col'), axis=0, tiled=True)  118 us
    all_to_all x1, blocking collectives, sent_and_summed(): lax.all_to_all(tiles, axis, split_axis=0, concat_axis=0, tiled=True)  28.4 us
    dot_general x1, matrix products, shards(): jnp.einsum('bgcm,gckmxy->bgkxy', place_cols, received, preferred_element_...  25.6 us
    dot_general x1, matrix products, shards(): jnp.einsum('agk,bgkxy->abxy', place_rows, gathered, preferred_element_typ...  18.8 us
    select_n x2, other arithmetic, shards(): by_both = jnp.take(by_rows, send_cols.reshape(-1), axis=2)  14.1 us
    all_to_all x1, starting transfers between devices, shards(): lax.all_to_all(outgoing, ('front', 'row', 'col'), split_axis=0, concat_ax...  11.1 us
  transfers between devices with their start and end apart: 2, of which 2 were waited for; matrix products, arithmetic and copies ran while one was open for 1% of the time, Pallas kernels for 0%

commit v1 on v0

--- a/solution.py
+++ b/solution.py
@@ -84,7 +84,10 @@
     share = row_span // n_col
     own_rows = lax.dynamic_slice_in_dim(border[0], col_index * share, share, 0)
     leaves = eliminate(pivot_block[0], own_rows, inverses[0])
-    factor = lax.all_gather(leaves, ("row", "col"), axis=0, tiled=True)
+    factor = jnp.concatenate(
+        lax.all_to_all(jnp.stack([leaves] * lax.axis_size(("row", "col"))), ("row", "col"), 0, 0),
+        axis=0,
+    )
     mine = lax.dynamic_slice_in_dim(factor, row_index * row_span, row_span, 0)
     theirs = lax.dynamic_slice_in_dim(factor, col_index * col_span, col_span, 0)
     update = (

time: 540 us -> 664 us (1.23)
  waiting for transfers between devices: 353 us -> 454 us
  starting transfers between devices: 11.1 us -> 35 us
  between operations: 14.5 us -> 1.4 us
    all_to_all x0 -> x1, waiting for transfers between devices: none -> 226 us  [shards(): lax.all_to_all(jnp.stack([leaves] * lax.axis_size(('row', 'col'))), ('row...]
    all_gather x1 -> x0, waiting for transfers between devices: 118 us -> none  [shards(): factor = lax.all_gather(leaves, ('row', 'col'), axis=0, tiled=True)]
    all_to_all x1, starting transfers between devices: 11.1 us -> 26.2 us  [shards(): lax.all_to_all(outgoing, ('front', 'row', 'col'), split_axis=0, concat_ax...]
    all_to_all x0 -> x1, starting transfers between devices: none -> 8.83 us  [shards(): lax.all_to_all(jnp.stack([leaves] * lax.axis_size(('row', 'col'))), ('row...]
    all_to_all x1, waiting for transfers between devices: 235 us -> 228 us  [shards(): lax.all_to_all(outgoing, ('front', 'row', 'col'), split_axis=0, concat_ax...]
where the time goes in v1:
time: 664 us; the launch traced here: 660 us
  waiting for transfers between devices  454 us (68%)
  matrix products  65.6 us (10%)
  local copies, waits for them, and re-layouts  44.8 us (7%)
  starting transfers between devices  35 us (5%)
  blocking collectives  32.1 us (5%)
  other arithmetic  27.2 us (4%)
    all_to_all x1, waiting for transfers between devices, shards(): lax.all_to_all(outgoing, ('front', 'row', 'col'), split_axis=0, concat_ax...  228 us
    all_to_all x1, waiting for transfers between devices, shards(): lax.all_to_all(jnp.stack([leaves] * lax.axis_size(('row', 'col'))), ('row...  226 us
    all_to_all x1, blocking collectives, sent_and_summed(): lax.all_to_all(tiles, axis, split_axis=0, concat_axis=0, tiled=True)  32.1 us
    all_to_all x1, starting transfers between devices, shards(): lax.all_to_all(outgoing, ('front', 'row', 'col'), split_axis=0, concat_ax...  26.2 us
    dot_general x1, matrix products, shards(): jnp.einsum('bgcm,gckmxy->bgkxy', place_cols, received, preferred_element_...  25.6 us
    dot_general x1, matrix products, shards(): jnp.einsum('agk,bgkxy->abxy', place_rows, gathered, preferred_element_typ...  18.9 us
    select_n x2, other arithmetic, shards(): by_both = jnp.take(by_rows, send_cols.reshape(-1), axis=2)  14.1 us
  transfers between devices with their start and end apart: 2, of which 2 were waited for; matrix products, arithmetic and copies ran while one was open for 1% of the time, Pallas kernels for 0%

profile of v1, /device:TPU:0, one launch (start us, length us, event | category | flops | bytes accessed | tf_op | source)
XLA Modules:
  0.0 660.1 jit_solution(2626341979953435082)
XLA Ops:
  0.7 1.2 dynamic-slice_bitcast_fusion
  1.9 1.1 convolution_convert_fusion.3
  3.1 1.4 fusion.19
  6.2 2.7 fusion.59
  10.1 2.2 fusion.22
  14.7 6.0 stack.2
  20.7 8.8 %all-to-all-start = ((bf16[32,256,1024]{2,1,0:T(8,128)(2,1)}), bf16[32,256,1024]{2,1,0:T(8,128)(2,1)}, u32[]{:S(2)}, u32[]{:S(2)}) async-start(bf16[32,256,1024]{2,1,0:T(8,128)(2,1)} %stack.2), calls=%async_computation | async-start | bytes 33554432 | tf_op jit(solution)/shard_map/all_to_all | solution.py:88
  29.6 1.9 gather_fusion
  32.7 1.9 gather_fusion.1
  36.2 226.2 %all-to-all-done = bf16[32,256,1024]{2,1,0:T(8,128)(2,1)} async-done(((bf16[32,256,1024]{2,1,0:T(8,128)(2,1)}), bf16[32,256,1024]{2,1,0:T(8,128)(2,1)}, u32[]{:S(2)}, u32[]{:S(2)}) %all-to-all-start) | async-done | bytes 16777248 | tf_op jit(solution)/shard_map/all_to_all | solution.py:88
  262.4 8.7 %fusion.8 = bf16[256,8,8,128]{3,1,2,0:T(8,128)(2,1)S(1)} fusion(bf16[1,2048,1024]{2,1,0:T(8,128)(2,1)} %param.11, bf16[8192,1024]{1,0:T(8,128)(2,1)} %bitcast.13, s32[]{:T(128)S(6)} %select_n.153, s32[]{:T(128)S(6)} %select_n.154), kind=kOutput, calls=%fused_computation.14 | convolution fusion | flops 4301258752 | bytes 14680072 | tf_op jit(solution)/shard_map/dot_general | solution.py:95
  271.1 3.1 copy.44
  274.1 7.2 %gather_fusion.2 = bf16[32,128,8,128]{3,2,1,0:T(8,128)(2,1)} fusion(bf16[16,128,8,128]{3,2,1,0:T(8,128)(2,1)} %bitcast.88, s32[1024]{0:T(1024)S(1)} %pad_clamp_fusion.1), kind=kCustom, calls=%fused_computation.2 | custom fusion | bytes 16777344 | tf_op jit(solution)/shard_map/jit(_take)/gather | solution.py:138
  281.3 7.5 %broadcast_select_fusion = bf16[32,128,8,128]{3,2,1,0:T(8,128)(2,1)} fusion(bf16[32,128,8,128]{3,2,1,0:T(8,128)(2,1)} %gather_fusion.2, pred[32]{0:T(512)(128)(4,1)S(1)} %compare_and_fusion.2), kind=kLoop, calls=%fused_computation.13 | loop fusion | flops 4194304 | bytes 16777248 | tf_op jit(solution)/shard_map/jit(_take)/select_n | solution.py:138
  288.8 8.8 %copy.31 = bf16[32,128,8,128]{3,1,0,2:T(8,128)(2,1)} copy(bf16[32,128,8,128]{3,2,1,0:T(8,128)(2,1)} %broadcast_select_fusion) | data formatting | bytes 16777216 | tf_op jit(solution)/shard_map/jit(_take)/select_n | solution.py:138
  297.6 10.4 %gather_fusion.3 = bf16[16,32,128,128]{3,2,1,0:T(8,128)(2,1)} fusion(bf16[32,128,8,128]{3,1,0,2:T(8,128)(2,1)} %copy.31, s32[1024]{0:T(1024)S(1)} %pad_clamp_fusion), kind=kCustom, calls=%fused_computation.3 | custom fusion | bytes 33554496 | tf_op jit(solution)/shard_map/jit(_take)/gather | solution.py:139
  308.0 14.1 %copy_select_fusion = bf16[16,2,128,8,2,128]{5,2,4,1,3,0:T(8,128)(2,1)} fusion(bf16[16,2,128,8,2,128]{5,2,1,0,4,3:T(8,128)(2,1)} %bitcast.87, pred[8,2]{1,0:T(8,128)(4,1)S(1)} %copy.26), kind=kLoop, calls=%fused_computation.8 | loop fusion | flops 8388608 | bytes 33554448 | tf_op jit(solution)/shard_map/jit(_take)/select_n | solution.py:139
  322.1 26.2 %all-to-all-start.1 = ((bf16[128,2,2,128,128]{4,3,2,1,0:T(8,128)(2,1)}), bf16[128,2,2,128,128]{4,3,2,1,0:T(8,128)(2,1)}, u32[]{:S(2)}, u32[]{:S(2)}) async-start(bf16[128,2,2,128,128]{4,3,2,1,0:T(8,128)(2,1)} %bitcast.86), calls=%async_computation.1 | async-start | bytes 33554432 | tf_op jit(solution)/shard_map/all_to_all | solution.py:144
  349.2 227.7 %all-to-all-done.1 = bf16[128,2,2,128,128]{4,3,2,1,0:T(8,128)(2,1)} async-done(((bf16[128,2,2,128,128]{4,3,2,1,0:T(8,128)(2,1)}), bf16[128,2,2,128,128]{4,3,2,1,0:T(8,128)(2,1)}, u32[]{:S(2)}, u32[]{:S(2)}) %all-to-all-start.1) | async-done | bytes 16777248 | tf_op jit(solution)/shard_map/all_to_all | solution.py:144
  577.0 25.6 %fusion = bf16[10,16,2,128,128]{4,0,3,2,1:T(8,128)(2,1)} fusion(bf16[10,16,8,2,1,1]{0,2,3,5,4,1:T(8,128)(2,1)S(1)} %bitcast.92, bf16[16,8,2,2,128,128]{5,4,3,2,1,0:T(8,128)(2,1)} %bitcast.20), kind=kOutput, calls=%fused_computation.5 | convolution fusion | flops 173015040 | bytes 27268096 | tf_op jit(solution)/shard_map/bgcm,gckmxy->bgkxy/dot_general | solution.py:148
  602.6 18.9 %fusion.11 = f32[5,128,10,128]{3,0,1,2:T(8,128)S(1)} fusion(bf16[10,16,2,128,128]{4,0,3,2,1:T(8,128)(2,1)} %fusion, bf16[5,16,2,1,1]{1,2,0,4,3:T(2,128)(2,1)S(1)} %convert_bitcast_fusion), kind=kOutput, calls=%fused_computation.19 | convolution fusion | flops 52428800 | bytes 13762880 | tf_op jit(solution)/shard_map/agk,bgkxy->abxy/dot_general | solution.py:151
  621.6 2.0 copy.37
  623.6 1.7 bitcast_add_fusion
  627.0 32.1 %all_to_all.15 = f32[8,80,512]{2,1,0:T(8,128)S(1)} all-to-all(f32[8,80,512]{2,1,0:T(8,128)S(1)} %bitcast.91), channel_id=1, replica_groups=mesh['front'=4,'row'=4,'col'=8] {'col'}, dimensions={0} | all-to-all | bytes 2621440 | tf_op jit(solution)/shard_map/all_to_all | solution.py:16
  (92 shorter events, 11.4 us)
Async XLA Ops:
  0.6 624.6 %copy-start = (bf16[1280,512]{1,0:T(8,128)(2,1)S(1)}, bf16[1280,512]{1,0:T(8,128)(2,1)}, u32[]{:S(2)}) copy-start(bf16[1280,512]{1,0:T(8,128)(2,1)} %param.17) | copy-start | bytes 3932164
  0.6 3.8 copy-start.4
  4.5 1.1 copy-start.6
  5.2 3.6 copy-start.2
  5.9 3.4 copy-start.7
  20.6 8.8 %copy-start.8 = (s32[4,64]{1,0:T(4,128)S(1)}, s32[4,64]{1,0:T(4,128)}, u32[]{:S(2)}) copy-start(s32[4,64]{1,0:T(4,128)} %param.14) | copy-start | bytes 3076
  20.6 8.9 %copy-start.9 = (s32[4,64]{1,0:T(4,128)S(1)}, s32[4,64]{1,0:T(4,128)}, u32[]{:S(2)}) copy-start(s32[4,64]{1,0:T(4,128)} %param.13) | copy-start | bytes 3076
  20.7 9.0 %copy-start.1 = (s32[80]{0:T(128)S(1)}, s32[80]{0:T(128)}, u32[]{:S(2)}) copy-start(s32[80]{0:T(128)} %param.15) | copy-start | bytes 964
  20.7 241.7 %all-to-all-start = ((bf16[32,256,1024]{2,1,0:T(8,128)(2,1)}), bf16[32,256,1024]{2,1,0:T(8,128)(2,1)}, u32[]{:S(2)}, u32[]{:S(2)}) async-start(bf16[32,256,1024]{2,1,0:T(8,128)(2,1)} %stack.2), calls=%async_computation | async-start | bytes 33554432 | tf_op jit(solution)/shard_map/all_to_all | solution.py:88
  322.1 254.9 %all-to-all-start.1 = ((bf16[128,2,2,128,128]{4,3,2,1,0:T(8,128)(2,1)}), bf16[128,2,2,128,128]{4,3,2,1,0:T(8,128)(2,1)}, u32[]{:S(2)}, u32[]{:S(2)}) async-start(bf16[128,2,2,128,128]{4,3,2,1,0:T(8,128)(2,1)} %bitcast.86), calls=%async_computation.1 | async-start | bytes 33554432 | tf_op jit(solution)/shard_map/all_to_all | solution.py:144
  621.6 2.0 copy-start.5
  625.3 1.7 copy-start.3
